TPU v7x, 32 devices: a whole 2x2x4 slice. The times are simulated.
32 devices in a mesh: rep: 2 (over x), mp: 16 (over z, y, core).
Axes of the slice: x: 2, y: 2, z: 4, core: 2. Of those that a mesh axis runs over, the one named last changes fastest.
Arguments:
- tokens: bfloat16 [1280, 3072], P(('rep', 'mp')), may hold values from -6 to 6
- w_in: bfloat16 [2, 3072, 2, 12288], P('rep', None, None, 'mp'), may hold values from -0.109375 to 0.109375
- w_down: bfloat16 [2, 12288, 3072], P('rep', 'mp'), may hold values from -0.0546875 to 0.0546875
- norm_gain: float32 [3072], replicated, may hold values from 0.1 to 1.9
- final_gain: float32 [3072], replicated, may hold values from 0.1 to 1.9
- value_head: float32 [3072], replicated, may hold values from -0.6 to 0.6
- owner: int32 [16], P('mp'), may hold values from 0 to 1
- lengths: int32 [16], P('rep'), may hold values from 20 to 80, as said below
- offsets: int32 [16], P('rep'), may hold values from 0 to 620, as said below
Outputs:
- mixed: bfloat16 [1280, 3072], P(('rep', 'mp'))
- rewards: float32 [16], P('rep')
Inputs may be any that keep to these rules, and one draw needn't show every extreme that they name: `lengths`: every rollout is at least a quarter of 80 long; in each group one rollout has exactly 80 tokens. `offsets`: rollout j of a group lies wholly within slots j * 80 to (j + 1) * 80 - 1 of its group; the other slots are padding.
All inputs are finite; a program needn't handle non-finite values.
Results may differ from a plain program's by a relative error of at most 0.0046.
Values may be sent and summed in bfloat16 or wider, within the bound.
A program may use at most 128 MiB of HBM per device.

v0:
```python
import jax
import jax.numpy as jnp
from jax import lax
from jax.sharding import PartitionSpec as P


def spread(value, axis, source):
    kept = jnp.where(lax.axis_index(axis) == source, value, 0).astype(value.dtype)
    return lax.psum(kept, axis)


def membership(slots, lengths, offsets):
    inside = (slots[:, None] >= offsets[None, :]) & (
        slots[:, None] < offsets[None, :] + lengths[None, :]
    )
    return inside.astype(jnp.float32)


def per_device(tokens, w_in, w_down, norm_gain, final_gain, value_head, owner, lengths, offsets):
    owner_index = owner[0]
    tok_rows = tokens.shape[0]
    width = tokens.shape[1]
    hidden_cols = w_in.shape[3]
    tokens_f = tokens.astype(jnp.float32)
    normed = (
        tokens_f
        * lax.rsqrt(jnp.mean(tokens_f * tokens_f, axis=1, keepdims=True) + 1e-06)
        * norm_gain
    ).astype(jnp.bfloat16)
    inner_local, outer_local = (
        spread(w_in, "rep", owner_index),
        spread(w_down, "rep", owner_index),
    )
    inner_matrix = inner_local.reshape(width, 2 * hidden_cols)
    piece = lax.all_gather(normed, "mp", axis=0, tiled=True)
    slots = jnp.arange(piece.shape[0], dtype=jnp.int32)
    row_count = piece.shape[0]
    products = jnp.dot(piece, inner_matrix, preferred_element_type=jnp.float32).reshape(
        row_count, 2, hidden_cols
    )
    gate_part = products[:, 0, :]
    up_part = products[:, 1, :]
    hidden = (
        jax.nn.gelu(gate_part, approximate=True)
        * up_part
        * jnp.sum(membership(slots, lengths, offsets), axis=1)[:, None]
    ).astype(jnp.bfloat16)
    outer_matrix = outer_local.reshape(hidden_cols, width)
    delta = lax.psum_scatter(
        jnp.dot(hidden, outer_matrix, preferred_element_type=jnp.float32),
        "mp",
        scatter_dimension=0,
        tiled=True,
    )
    resid = tokens_f + delta
    mixed = resid.astype(jnp.bfloat16)
    final = resid * lax.rsqrt(jnp.mean(resid * resid, axis=1, keepdims=True) + 1e-06) * final_gain
    values = jnp.dot(final, value_head, precision=lax.Precision.HIGHEST)
    own_slots = lax.axis_index("mp") * tok_rows + jnp.arange(tok_rows, dtype=jnp.int32)
    member = membership(own_slots, lengths, offsets)
    partial_sums = jnp.dot(values, member, precision=lax.Precision.HIGHEST)
    totals = lax.psum(partial_sums, "mp")
    rewards = totals / lengths.astype(jnp.float32)
    return (mixed, rewards)


def solution(mesh):
    in_specs = (
        P(("rep", "mp"), None),
        P("rep", None, None, "mp"),
        P("rep", "mp", None),
        P(),
        P(),
        P(),
        P("mp"),
        P("rep"),
        P("rep"),
    )
    out_specs = (P(("rep", "mp"), None), P("rep"))
    return jax.shard_map(
        per_device, mesh=mesh, in_specs=in_specs, out_specs=out_specs, check_vma=False
    )
```

profile of v0, /device:TPU:0, one launch (start us, length us, event | category | flops | bytes accessed | tf_op | source)
XLA Modules:
  0.0 530.3 jit_solution(2742017542717599871)
XLA Ops:
  8.0 0.0 copy-start
  8.0 0.0 all-gather.2.cloned.1.call-start
  8.1 1.1 fusion.19
  9.2 1.8 fusion.21
  10.9 0.0 all-gather.2.cloned.1.call-update
  11.0 0.0 all-reduce.3.cloned.1.call-start
  11.7 9.3 %broadcast_select_fusion = bf16[1,3072,2,768]{3,2,1,0:T(2,128)(2,1)} fusion(bf16[1,3072,2,768]{3,2,1,0:T(2,128)(2,1)} %param.10, pred[]{:T(512)S(6)} %eq.4), kind=kLoop, calls=%fused_computation | loop fusion | flops 4718592 | bytes 18874368 | tf_op jit(solution)/shard_map/jit(_where)/select_n | solution.py:8
  20.9 23.8 %copy.13 = bf16[1,3072,2,768]{1,3,2,0:T(8,128)(2,1)} copy(bf16[1,3072,2,768]{3,2,1,0:T(2,128)(2,1)} %broadcast_select_fusion) | data formatting | bytes 18874368 | tf_op jit(solution)/shard_map/reshape | solution.py:34
  44.7 2.6 select_bitcast_fusion
  47.3 0.0 copy-start.3
  47.3 0.0 copy-start.5
  47.3 0.0 all-reduce.3.cloned.1.call-update
  47.3 0.0 reduce-scatter.2.cloned.1.call-start
  47.4 0.6 copy-done.3
  47.9 0.0 copy-done.5
  48.0 0.1 convert_reduce_fusion
  48.1 15.4 %all-gather.2.cloned.1.call-done = bf16[640,3072]{1,0:T(8,128)(2,1)} async-done(((bf16[40,3072]{1,0:T(8,128)(2,1)}), bf16[640,3072]{1,0:T(8,128)(2,1)}) %all-gather.2.cloned.1.call-update) | async-done | bytes 3932176 | tf_op jit(solution)/shard_map/all_gather | solution.py:35
  63.5 311.1 %all-reduce.3.cloned.1.call-done = (bf16[768,3072]{1,0:T(8,128)(2,1)}, bf16[2,768,3072]{2,1,0:T(8,128)(2,1)}) async-done(((bf16[768,3072]{1,0:T(8,128)(2,1)}, bf16[2,768,3072]{2,1,0:T(8,128)(2,1)}), (bf16[768,3072]{1,0:T(8,128)(2,1)}, bf16[2,768,3072]{2,1,0:T(8,128)(2,1)})) %all-reduce.3.cloned.1.call-update) | async-done | bytes 14155792 | tf_op jit(solution)/shard_map/psum | solution.py:9
  374.6 0.0 copy-start.4
  374.6 10.2 %fusion = f32[640,2,768]{2,0,1:T(8,128)S(1)} fusion(bf16[2,768,3072]{2,1,0:T(8,128)(2,1)} %get-tuple-element.3, bf16[640,3072]{1,0:T(8,128)(2,1)} %all-gather.2.cloned.1.call-done), kind=kOutput, calls=%fused_computation.2 | convolution fusion | flops 6039797760 | bytes 17301504 | tf_op jit(solution)/shard_map/dot_general | solution.py:38
  384.8 0.0 copy-done.4
  384.8 6.4 %fusion.12 = f32[640,3072]{1,0:T(8,128)} fusion(bf16[768,3072]{1,0:T(8,128)(2,1)S(1)} %copy-done.4, f32[640,2,768]{2,0,1:T(8,128)S(1)} %fusion, f32[640]{0:T(1024)S(1)} %convert_reduce_fusion), kind=kOutput, calls=%fused_computation.17 | convolution fusion | flops 3025305600 | bytes 16517632 | tf_op jit(solution)/shard_map/dot_general | solution.py:50
  391.1 0.0 reduce-scatter.2.cloned.1.call-update
  391.2 95.3 %reduce-scatter.2.cloned.1.call-done = f32[40,3072]{1,0:T(8,128)} async-done(((f32[640,3072]{1,0:T(8,128)}), f32[40,3072]{1,0:T(8,128)}) %reduce-scatter.2.cloned.1.call-update) | async-done | bytes 491536 | tf_op jit(solution)/shard_map/reduce_scatter | solution.py:49
  486.5 0.0 copy-done.1
  486.5 1.9 multiply_reduce_fusion
  488.4 0.0 copy-done
  488.4 0.0 copy-done.2
  488.4 1.6 convolution_bitcast_fusion.1
  490.1 0.2 convolution_bitcast_fusion
  490.3 32.1 %psum.23 = f32[8]{0:T(128)S(1)} all-reduce(f32[8]{0:T(128)S(1)} %convolution_bitcast_fusion), channel_id=1, replica_groups=mesh['rep'=2,'mp'=16] {'mp'}, use_global_device_ids=true, to_apply=%region_6.7 | all-reduce | flops 8 | bytes 64 | tf_op jit(solution)/shard_map/psum | solution.py:62
  522.3 0.5 convert_divide_fusion
  (6 shorter events, 0.0 us)
Async XLA Ops:
  8.0 480.4 %copy-start = (f32[3072]{0:T(1024)S(1)}, f32[3072]{0:T(1024)}, u32[]{:S(2)}) copy-start(f32[3072]{0:T(1024)} %param.14) | copy-start | bytes 36868
  8.0 55.5 %all-gather.2.cloned.1.call-start = ((), (), s32[]{:S(2)}) async-start(), calls=%async_computation.1 | async-start | bytes 4177920 | tf_op jit(solution)/shard_map/all_gather | solution.py:35
  11.0 363.6 %all-reduce.3.cloned.1.call-start = ((), (), s32[]{:S(2)}) async-start(), calls=%async_computation.3 | async-start | bytes 28311552 | tf_op jit(solution)/shard_map/psum | solution.py:9
  47.3 0.7 copy-start.3
  47.3 0.7 copy-start.5
  47.3 439.2 %reduce-scatter.2.cloned.1.call-start = ((), (), s32[]{:S(2)}) async-start(), calls=%async_computation.2 | async-start | bytes 8355840 | tf_op jit(solution)/shard_map/reduce_scatter | solution.py:49
  374.6 10.2 %copy-start.4 = (bf16[768,3072]{1,0:T(8,128)(2,1)S(1)}, bf16[768,3072]{1,0:T(8,128)(2,1)}, u32[]{:S(2)}) copy-start(bf16[768,3072]{1,0:T(8,128)(2,1)} %get-tuple-element.2) | copy-start | bytes 14155780
  391.1 95.4 %copy-start.1 = (bf16[40,3072]{1,0:T(8,128)(2,1)S(1)}, bf16[40,3072]{1,0:T(8,128)(2,1)}, u32[]{:S(2)}) copy-start(bf16[40,3072]{1,0:T(8,128)(2,1)} %param.9) | copy-start | bytes 737284
  391.1 97.3 %copy-start.2 = (f32[3072]{0:T(1024)S(1)}, f32[3072]{0:T(1024)}, u32[]{:S(2)}) copy-start(f32[3072]{0:T(1024)} %param.13) | copy-start | bytes 36868
Sparse Core Ops, SparseCore 0:
  11.7 51.7 all-gather.1
  391.3 95.1 reduce-scatter.1
Sparse Core Ops, SparseCore 1:
  47.4 327.1 all-reduce.2
where the time goes:
time: 531 us; the launch traced here: 530 us
  waiting for transfers between devices  422 us (79%)
  blocking collectives  32.1 us (6%)
  local copies, waits for them, and re-layouts  24.4 us (5%)
  matrix products  18.4 us (3%)
  other arithmetic  17.2 us (3%)
  between operations  16.2 us (3%)
    psum x1, waiting for transfers between devices, spread(): return lax.psum(kept, axis)  311 us
    reduce_scatter x1, waiting for transfers between devices, per_device(): lax.psum_scatter(jnp.dot(hidden, outer_matrix, preferred_element_type=jnp...  95.3 us
    psum x1, blocking collectives, per_device(): totals = lax.psum(partial_sums, 'mp')  32.1 us
    reshape x1, local copies, waits for them, and re-layouts, per_device(): inner_matrix = inner_local.reshape(width, 2 * hidden_cols)  23.8 us
    all_gather x1, waiting for transfers between devices, per_device(): piece = lax.all_gather(normed, 'mp', axis=0, tiled=True)  15.4 us
  transfers between devices with their start and end apart: 3, of which 3 were waited for; matrix products, arithmetic and copies ran while one was open for 7% of the time, Pallas kernels for 0%

commit v1 on v0

--- a/solution.py
+++ b/solution.py
@@ -6,7 +6,7 @@
 
 def spread(value, axis, source):
     kept = jnp.where(lax.axis_index(axis) == source, value, 0).astype(value.dtype)
-    return lax.psum(kept, axis)
+    return jnp.sum(lax.all_gather(kept, axis), axis=0)
 
 
 def membership(slots, lengths, offsets):

time: 531 us -> 565 us (1.064)
  other arithmetic: 17.2 us -> 41.7 us
  waiting for transfers between devices: 422 us -> 436 us
    all_gather x0 -> x2, waiting for transfers between devices: none -> 328 us  [spread(): return jnp.sum(lax.all_gather(kept, axis), axis=0)]
    psum x1 -> x0, waiting for transfers between devices: 311 us -> none  [spread(): return lax.psum(kept, axis)]
    reduce_sum x0 -> x2, other arithmetic: none -> 27.2 us  [spread(): return jnp.sum(lax.all_gather(kept, axis), axis=0)]
    reshape x1, local copies, waits for them, and re-layouts: 23.8 us -> 8.12 us  [per_device(): inner_matrix = inner_local.reshape(width, 2 * hidden_cols)]
    dot_general x0 -> x1, local copies, waits for them, and re-layouts: none -> 12.6 us  [per_device(): jnp.dot(piece, inner_matrix, preferred_element_type=jnp.float32)]
  transfers between devices with their start and end apart: 3 -> 4, of which waited for: 3 -> 4; matrix products, arithmetic and copies ran while one was open for 7% -> 10% of each run, Pallas kernels for 0% -> 0%
where the time goes in v1:
time: 565 us; the launch traced here: 564 us
  waiting for transfers between devices  436 us (77%)
  other arithmetic  41.7 us (7%)
  blocking collectives  32.1 us (6%)
  local copies, waits for them, and re-layouts  21.6 us (4%)
  matrix products  18.3 us (3%)
  between operations  14.5 us (3%)
    all_gather x2, waiting for transfers between devices, spread(): return jnp.sum(lax.all_gather(kept, axis), axis=0)  328 us
    reduce_scatter x1, waiting for transfers between devices, per_device(): lax.psum_scatter(jnp.dot(hidden, outer_matrix, preferred_element_type=jnp...  93.9 us
    psum x1, blocking collectives, per_device(): totals = lax.psum(partial_sums, 'mp')  32.1 us
    reduce_sum x2, other arithmetic, spread(): return jnp.sum(lax.all_gather(kept, axis), axis=0)  27.2 us
    all_gather x1, waiting for transfers between devices, per_device(): piece = lax.all_gather(normed, 'mp', axis=0, tiled=True)  14.3 us
    dot_general x1, local copies, waits for them, and re-layouts, per_device(): jnp.dot(piece, inner_matrix, preferred_element_type=jnp.float32)  12.6 us
  transfers between devices with their start and end apart: 4, of which 4 were waited for; matrix products, arithmetic and copies ran while one was open for 10% of the time, Pallas kernels for 0%

profile of v1, /device:TPU:0, one launch (start us, length us, event | category | flops | bytes accessed | tf_op | source)
XLA Modules:
  0.0 564.4 jit_solution(12748305023824948952)
XLA Ops:
  7.2 0.0 copy-start
  7.2 0.0 all-gather.10.cloned.1.call-start
  7.9 2.5 broadcast_select_fusion
  10.3 0.0 all-gather.10.cloned.1.call-update
  10.4 0.0 all-gather.8.cloned.1.call-start
  10.4 8.5 %copy_select_fusion = bf16[1,3072,2,768]{3,1,2,0:T(8,128)(2,1)} fusion(bf16[1,3072,2,768]{3,2,1,0:T(2,128)(2,1)} %param.10, pred[]{:T(512)S(6)} %eq.4), kind=kLoop, calls=%fused_computation | loop fusion | flops 4718592 | bytes 18874368 | tf_op jit(solution)/shard_map/jit(_where)/select_n | solution.py:8
  19.0 0.0 all-gather.8.cloned.1.call-update
  19.0 0.0 all-gather.6.cloned.1.call-start
  19.1 0.9 copy-done.1
  19.9 0.2 fusion.19
  20.1 0.0 copy-done.2
  20.1 0.8 fusion.21
  20.9 0.0 all-gather.6.cloned.1.call-update
  20.9 0.0 reduce-scatter.2.cloned.1.call-start
  21.0 0.0 copy-done.4
  21.0 0.1 convert_reduce_fusion
  21.1 111.9 %all-gather.10.cloned.1.call-done = bf16[2,768,3072]{2,1,0:T(8,128)(2,1)} async-done(((bf16[1,768,3072]{2,1,0:T(8,128)(2,1)}), bf16[2,768,3072]{2,1,0:T(8,128)(2,1)}) %all-gather.10.cloned.1.call-update) | async-done | bytes 9437200 | tf_op jit(solution)/shard_map/all_gather | solution.py:9
  133.0 10.4 %reduce.5 = bf16[768,3072]{1,0:T(8,128)(2,1)} reduce(bf16[2,768,3072]{2,1,0:T(8,128)(2,1)} %all-gather.10.cloned.1.call-done, bf16[]{:T(256)} %constant.25.clone.1), dimensions={0}, to_apply=%region_3.4 | reduce | flops 2359296 | bytes 14155778 | tf_op jit(solution)/shard_map/reduce_sum | solution.py:9
  143.4 215.6 %all-gather.8.cloned.1.call-done = bf16[2,3072,2,768]{3,1,2,0:T(8,128)(2,1)} async-done(((bf16[1,3072,2,768]{3,1,2,0:T(8,128)(2,1)}), bf16[2,3072,2,768]{3,1,2,0:T(8,128)(2,1)}) %all-gather.8.cloned.1.call-update) | async-done | bytes 18874384 | tf_op jit(solution)/shard_map/all_gather | solution.py:9
  359.0 16.8 %reduce.4 = bf16[3072,2,768]{2,0,1:T(8,128)(2,1)} reduce(bf16[2,3072,2,768]{3,1,2,0:T(8,128)(2,1)} %all-gather.8.cloned.1.call-done, bf16[]{:T(256)} %constant.25.clone.1), dimensions={0}, to_apply=%region_1.2 | reduce | flops 4718592 | bytes 28311554 | tf_op jit(solution)/shard_map/reduce_sum | solution.py:9
  375.9 8.1 %copy.18 = bf16[2,384,8,768]{3,2,0,1:T(8,128)(2,1)} copy(bf16[2,384,8,768]{3,2,1,0:T(8,128)(2,1)} %bitcast.25) | data formatting | bytes 18874368 | tf_op jit(solution)/shard_map/reshape | solution.py:34
  384.0 12.6 %copy.16 = bf16[1536,3072]{1,0:T(8,128)(2,1)} copy(bf16[1536,3072]{0,1:T(8,128)(2,1)} %bitcast.24) | data formatting | bytes 18874368 | tf_op jit(solution)/shard_map/dot_general | solution.py:38
  396.6 14.3 %all-gather.6.cloned.1.call-done = bf16[640,3072]{1,0:T(8,128)(2,1)} async-done(((bf16[40,3072]{1,0:T(8,128)(2,1)}), bf16[640,3072]{1,0:T(8,128)(2,1)}) %all-gather.6.cloned.1.call-update) | async-done | bytes 3932176 | tf_op jit(solution)/shard_map/all_gather | solution.py:35
  411.0 10.2 %fusion = f32[640,2,768]{2,0,1:T(8,128)S(1)} fusion(bf16[2,768,3072]{2,1,0:T(8,128)(2,1)} %bitcast.26, bf16[640,3072]{1,0:T(8,128)(2,1)} %all-gather.6.cloned.1.call-done), kind=kOutput, calls=%fused_computation.2 | convolution fusion | flops 6039797760 | bytes 17301504 | tf_op jit(solution)/shard_map/dot_general | solution.py:38
  421.2 6.3 %fusion.12 = f32[640,3072]{1,0:T(8,128)} fusion(bf16[768,3072]{1,0:T(8,128)(2,1)S(1)} %bitcast.28, f32[640,2,768]{2,0,1:T(8,128)S(1)} %fusion, f32[640]{0:T(1024)S(1)} %convert_reduce_fusion), kind=kOutput, calls=%fused_computation.17 | convolution fusion | flops 3025305600 | bytes 16517632 | tf_op jit(solution)/shard_map/dot_general | solution.py:50
  427.5 0.0 reduce-scatter.2.cloned.1.call-update
  427.6 93.9 %reduce-scatter.2.cloned.1.call-done = f32[40,3072]{1,0:T(8,128)} async-done(((f32[640,3072]{1,0:T(8,128)}), f32[40,3072]{1,0:T(8,128)}) %reduce-scatter.2.cloned.1.call-update) | async-done | bytes 491536 | tf_op jit(solution)/shard_map/reduce_scatter | solution.py:49
  521.5 1.9 multiply_reduce_fusion
  523.5 1.6 convolution_bitcast_fusion.1
  525.1 0.2 convolution_bitcast_fusion
  525.3 32.1 %psum.7 = f32[8]{0:T(128)S(1)} all-reduce(f32[8]{0:T(128)S(1)} %convolution_bitcast_fusion), channel_id=1, replica_groups=mesh['rep'=2,'mp'=16] {'mp'}, use_global_device_ids=true, to_apply=%region_6.7 | all-reduce | flops 8 | bytes 64 | tf_op jit(solution)/shard_map/psum | solution.py:62
  557.4 0.5 convert_divide_fusion
  (17 shorter events, 0.0 us)
Async XLA Ops:
  7.2 516.3 %copy-start = (f32[3072]{0:T(1024)S(1)}, f32[3072]{0:T(1024)}, u32[]{:S(2)}) copy-start(f32[3072]{0:T(1024)} %param.14) | copy-start | bytes 36868
  7.2 125.9 %all-gather.10.cloned.1.call-start = ((), (), s32[]{:S(2)}) async-start(), calls=%async_computation.4 | async-start | bytes 14155776 | tf_op jit(solution)/shard_map/all_gather | solution.py:9
  10.4 348.7 %all-gather.8.cloned.1.call-start = ((), (), s32[]{:S(2)}) async-start(), calls=%async_computation.3 | async-start | bytes 28311552 | tf_op jit(solution)/shard_map/all_gather | solution.py:9
  19.0 0.9 copy-start.1
  19.0 1.1 copy-start.2
  19.0 2.0 copy-start.4
  19.0 2.0 copy-start.5
  19.0 392.0 %all-gather.6.cloned.1.call-start = ((), (), s32[]{:S(2)}) async-start(), calls=%async_computation.1 | async-start | bytes 4177920 | tf_op jit(solution)/shard_map/all_gather | solution.py:35
  20.9 500.6 %reduce-scatter.2.cloned.1.call-start = ((), (), s32[]{:S(2)}) async-start(), calls=%async_computation.2 | async-start | bytes 8355840 | tf_op jit(solution)/shard_map/reduce_scatter | solution.py:49
  384.0 37.2 %slice-start = ((s8[4718592]{0:T(1024)(128)(4,1)}), s8[524288]{0:T(1024)(128)(4,1)S(1)}, s32[]{:S(2)}) async-start(s8[4718592]{0:T(1024)(128)(4,1)} %bitcast.27), calls=%async_computation.5 | async-start | bytes 1048576
  411.0 10.2 %slice-start.1 = ((s8[4718592]{0:T(1024)(128)(4,1)}), s8[4194304]{0:T(1024)(128)(4,1)S(1)}, s32[]{:S(2)}) async-start(s8[4718592]{0:T(1024)(128)(4,1)} %bitcast.27), calls=%async_computation.6 | async-start | bytes 8388608
  427.5 95.9 %copy-start.3 = (f32[3072]{0:T(1024)S(1)}, f32[3072]{0:T(1024)}, u32[]{:S(2)}) copy-start(f32[3072]{0:T(1024)} %param.13) | copy-start | bytes 36868
Sparse Core Ops, SparseCore 0:
  10.5 122.5 all-gather.9
  134.6 224.3 all-gather.7
  361.9 49.0 all-gather.5
  427.7 93.7 reduce-scatter.1

commit v2 on v0

--- a/solution.py
+++ b/solution.py
@@ -59,7 +59,7 @@
     own_slots = lax.axis_index("mp") * tok_rows + jnp.arange(tok_rows, dtype=jnp.int32)
     member = membership(own_slots, lengths, offsets)
     partial_sums = jnp.dot(values, member, precision=lax.Precision.HIGHEST)
-    totals = lax.psum(partial_sums, "mp")
+    totals = jnp.sum(lax.all_gather(partial_sums, "mp"), axis=0)
     rewards = totals / lengths.astype(jnp.float32)
     return (mixed, rewards)
 

time: 531 us -> 532 us (level)
    psum x1 -> x0, blocking collectives: 32.1 us -> none  [per_device(): totals = lax.psum(partial_sums, 'mp')]
    unnamed x0 -> x1, blocking collectives: none -> 32.1 us
where the time goes in v2:
time: 532 us; the launch traced here: 531 us
  waiting for transfers between devices  420 us (79%)
  blocking collectives  32.1 us (6%)
  local copies, waits for them, and re-layouts  25.9 us (5%)
  matrix products  18.4 us (3%)
  other arithmetic  17.3 us (3%)
  between operations  16.9 us (3%)
    psum x1, waiting for transfers between devices, spread(): return lax.psum(kept, axis)  311 us
    reduce_scatter x1, waiting for transfers between devices, per_device(): lax.psum_scatter(jnp.dot(hidden, outer_matrix, preferred_element_type=jnp...  93.5 us
    unnamed x1, blocking collectives  32.1 us
    reshape x1, local copies, waits for them, and re-layouts, per_device(): inner_matrix = inner_local.reshape(width, 2 * hidden_cols)  23.8 us
    all_gather x1, waiting for transfers between devices, per_device(): piece = lax.all_gather(normed, 'mp', axis=0, tiled=True)  15.4 us
  transfers between devices with their start and end apart: 3, of which 3 were waited for; matrix products, arithmetic and copies ran while one was open for 7% of the time, Pallas kernels for 0%

profile of v2, /device:TPU:0, one launch (start us, length us, event | category | flops | bytes accessed | tf_op | source)
XLA Modules:
  0.0 530.7 jit_solution(16054112863221707681)
XLA Ops:
  8.0 0.0 copy-start
  8.0 0.0 all-gather.3.cloned.1.call-start
  8.1 1.1 fusion.19
  9.2 1.8 fusion.21
  10.9 0.0 all-gather.3.cloned.1.call-update
  11.0 0.0 all-reduce.4.cloned.1.call-start
  11.7 9.3 %broadcast_select_fusion = bf16[1,3072,2,768]{3,2,1,0:T(2,128)(2,1)} fusion(bf16[1,3072,2,768]{3,2,1,0:T(2,128)(2,1)} %param.10, pred[]{:T(512)S(6)} %eq.4), kind=kLoop, calls=%fused_computation | loop fusion | flops 4718592 | bytes 18874368 | tf_op jit(solution)/shard_map/jit(_where)/select_n | solution.py:8
  20.9 23.8 %copy.14 = bf16[1,3072,2,768]{1,3,2,0:T(8,128)(2,1)} copy(bf16[1,3072,2,768]{3,2,1,0:T(2,128)(2,1)} %broadcast_select_fusion) | data formatting | bytes 18874368 | tf_op jit(solution)/shard_map/reshape | solution.py:34
  44.8 2.6 select_bitcast_fusion
  47.3 0.0 all-reduce.4.cloned.1.call-update
  47.4 0.0 reduce-scatter.2.cloned.1.call-start
  47.4 0.6 copy-done.3
  48.0 0.0 copy-done.5
  48.0 0.1 convert_reduce_fusion
  48.1 15.4 %all-gather.3.cloned.1.call-done = bf16[640,3072]{1,0:T(8,128)(2,1)} async-done(((bf16[40,3072]{1,0:T(8,128)(2,1)}), bf16[640,3072]{1,0:T(8,128)(2,1)}) %all-gather.3.cloned.1.call-update) | async-done | bytes 3932176 | tf_op jit(solution)/shard_map/all_gather | solution.py:35
  63.5 311.1 %all-reduce.4.cloned.1.call-done = (bf16[768,3072]{1,0:T(8,128)(2,1)}, bf16[2,768,3072]{2,1,0:T(8,128)(2,1)}) async-done(((bf16[768,3072]{1,0:T(8,128)(2,1)}, bf16[2,768,3072]{2,1,0:T(8,128)(2,1)}), (bf16[768,3072]{1,0:T(8,128)(2,1)}, bf16[2,768,3072]{2,1,0:T(8,128)(2,1)})) %all-reduce.4.cloned.1.call-update) | async-done | bytes 14155792 | tf_op jit(solution)/shard_map/psum | solution.py:9
  374.6 10.2 %fusion = f32[640,2,768]{2,0,1:T(8,128)S(1)} fusion(bf16[2,768,3072]{2,1,0:T(8,128)(2,1)} %get-tuple-element.3, bf16[640,3072]{1,0:T(8,128)(2,1)} %all-gather.3.cloned.1.call-done), kind=kOutput, calls=%fused_computation.2 | convolution fusion | flops 6039797760 | bytes 17301504 | tf_op jit(solution)/shard_map/dot_general | solution.py:38
  384.8 0.0 copy-done.4
  384.8 6.4 %fusion.12 = f32[640,3072]{1,0:T(8,128)} fusion(bf16[768,3072]{1,0:T(8,128)(2,1)S(1)} %copy-done.4, f32[640,2,768]{2,0,1:T(8,128)S(1)} %fusion, f32[640]{0:T(1024)S(1)} %convert_reduce_fusion), kind=kOutput, calls=%fused_computation.17 | convolution fusion | flops 3025305600 | bytes 16517632 | tf_op jit(solution)/shard_map/dot_general | solution.py:50
  391.2 0.0 reduce-scatter.2.cloned.1.call-update
  391.2 0.6 copy-done.6
  391.9 0.6 dynamic-slice
  393.1 93.5 %reduce-scatter.2.cloned.1.call-done = f32[40,3072]{1,0:T(8,128)} async-done(((f32[640,3072]{1,0:T(8,128)}), f32[40,3072]{1,0:T(8,128)}) %reduce-scatter.2.cloned.1.call-update) | async-done | bytes 491536 | tf_op jit(solution)/shard_map/reduce_scatter | solution.py:49
  486.6 0.0 copy-done.1
  486.6 1.9 multiply_reduce_fusion
  488.5 0.0 copy-done
  488.5 1.6 convolution_bitcast_fusion.1
  490.1 0.2 convolution_bitcast_fusion
  490.3 0.2 dynamic-update-slice
  490.5 32.1 %all-reduce = f32[128]{0:T(128)S(1)} all-reduce(f32[128]{0:T(128)S(1)} %dynamic-update-slice), channel_id=2, replica_groups=mesh['rep'=2,'mp'=16] {'mp'}, use_global_device_ids=true, to_apply=%add | all-reduce | flops 128 | bytes 1024
  522.6 0.1 reshape.46
  522.7 0.5 convert_divide_fusion
  (13 shorter events, 0.1 us)
Async XLA Ops:
  8.0 480.5 %copy-start = (f32[3072]{0:T(1024)S(1)}, f32[3072]{0:T(1024)}, u32[]{:S(2)}) copy-start(f32[3072]{0:T(1024)} %param.14) | copy-start | bytes 36868
  8.0 55.5 %all-gather.3.cloned.1.call-start = ((), (), s32[]{:S(2)}) async-start(), calls=%async_computation.1 | async-start | bytes 4177920 | tf_op jit(solution)/shard_map/all_gather | solution.py:35
  11.0 363.6 %all-reduce.4.cloned.1.call-start = ((), (), s32[]{:S(2)}) async-start(), calls=%async_computation.3 | async-start | bytes 28311552 | tf_op jit(solution)/shard_map/psum | solution.py:9
  47.3 0.7 copy-start.3
  47.3 0.7 copy-start.5
  47.4 439.2 %reduce-scatter.2.cloned.1.call-start = ((), (), s32[]{:S(2)}) async-start(), calls=%async_computation.2 | async-start | bytes 8355840 | tf_op jit(solution)/shard_map/reduce_scatter | solution.py:49
  374.6 10.2 %copy-start.4 = (bf16[768,3072]{1,0:T(8,128)(2,1)S(1)}, bf16[768,3072]{1,0:T(8,128)(2,1)}, u32[]{:S(2)}) copy-start(bf16[768,3072]{1,0:T(8,128)(2,1)} %get-tuple-element.2) | copy-start | bytes 14155780
  391.2 0.7 copy-start.6
  391.2 95.4 %copy-start.1 = (bf16[40,3072]{1,0:T(8,128)(2,1)S(1)}, bf16[40,3072]{1,0:T(8,128)(2,1)}, u32[]{:S(2)}) copy-start(bf16[40,3072]{1,0:T(8,128)(2,1)} %param.9) | copy-start | bytes 737284
  391.2 97.3 %copy-start.2 = (f32[3072]{0:T(1024)S(1)}, f32[3072]{0:T(1024)}, u32[]{:S(2)}) copy-start(f32[3072]{0:T(1024)} %param.13) | copy-start | bytes 36868
Sparse Core Ops, SparseCore 0:
  11.7 51.7 all-gather.2
  391.4 95.1 reduce-scatter.1
Sparse Core Ops, SparseCore 1:
  47.4 327.1 all-reduce.3
